TPU v7x, 32 devices: a whole 2x2x4 slice. The times are simulated.
32 devices in a mesh: rep: 4 (over x, y), pp: 8 (over z, core).
Axes of the slice: x: 2, y: 2, z: 4, core: 2. Of those that a mesh axis runs over, the one named last changes fastest.
Arguments:
- x: bfloat16 [64, 512, 512], P('rep'), parts along dimension 0
- dy: bfloat16 [64, 512, 512], P('rep'), parts along dimension 0
- w_gate: bfloat16 [8, 512, 1792], P('pp')
- w_up: bfloat16 [8, 512, 1792], P('pp')
- w_down: bfloat16 [8, 1792, 512], P('pp')
Outputs:
- output 1: bfloat16 [32, 512, 1792], P(('rep', 'pp')), parts along dimension 0
- output 2: bfloat16 [32, 512, 1792], P(('rep', 'pp')), parts along dimension 0
- output 3: bfloat16 [32, 1792, 512], P(('rep', 'pp')), parts along dimension 0
There are 4 independent parts. A program takes and returns all parts, laid end to end along the dimension named above; an argument that names none is the same for every part.
All inputs are finite; a program needn't handle non-finite values.
Results may differ from a plain program's by a relative error of at most 0.029.
Values are sent between devices in bfloat16 or wider.
A program may use at most 2 GiB of HBM per device.

v0:
```python
import jax
import jax.numpy as jnp
from jax import lax
from jax.sharding import PartitionSpec as P

NAMES = ("w_gate", "w_up", "w_down")


def matmul(a, w):
    return jnp.dot(a, w, preferred_element_type=jnp.float32).astype(jnp.bfloat16)


def normed(h):
    wide = h.astype(jnp.float32)
    scale = lax.rsqrt(jnp.mean(wide**2, -1, keepdims=True) + 1e-6)
    return (wide * scale).astype(jnp.bfloat16)


def layer(h, w):
    a = normed(h)
    gate = jnp.dot(a, w["w_gate"], preferred_element_type=jnp.float32)
    up = jnp.dot(a, w["w_up"], preferred_element_type=jnp.float32)
    return h + matmul((jax.nn.silu(gate) * up).astype(jnp.bfloat16), w["w_down"])


def stage(weights, h):
    for number in range(weights["w_gate"].shape[0]):
        h = layer(h, {name: w[number] for name, w in weights.items()})
    return h


def solution(mesh):
    stages = mesh.shape["pp"]
    onward = [(i, i + 1) for i in range(stages - 1)]
    back_again = [(i + 1, i) for i in range(stages - 1)]

    def step(x, dy, *arrays):
        weights = dict(zip(NAMES, arrays, strict=True))
        micro, me = x.shape[0], lax.axis_index("pp")
        kept, came = jnp.zeros_like(x), jnp.zeros_like(x[0])
        for t in range(micro + stages - 1):
            number = jnp.clip(t - me, 0, micro - 1)
            at_work = (t >= me) & (t - me < micro)
            h = jnp.where(me == 0, x[min(t, micro - 1)], came)
            was = lax.dynamic_index_in_dim(kept, number, 0, keepdims=False)
            kept = lax.dynamic_update_index_in_dim(kept, jnp.where(at_work, h, was), number, 0)
            came = lax.ppermute(stage(weights, h), "pp", onward)
        total = {name: jnp.zeros(w.shape, jnp.float32) for name, w in weights.items()}
        came, behind = jnp.zeros_like(x[0]), stages - 1 - me
        for t in range(micro + stages - 1):
            number = jnp.clip(t - behind, 0, micro - 1)
            at_work = (t >= behind) & (t - behind < micro)
            by_y = jnp.where(behind == 0, dy[min(t, micro - 1)], came)
            _, back = jax.vjp(stage, weights, lax.dynamic_index_in_dim(kept, number, 0, keepdims=False))
            by_w, by_h = back(by_y)
            total = {name: total[name] + jnp.where(at_work, by_w[name].astype(jnp.float32), 0.0) for name in NAMES}
            came = lax.ppermute(by_h, "pp", back_again)
        return tuple(total[name].astype(jnp.bfloat16) for name in NAMES)

    return jax.shard_map(
        step,
        mesh=mesh,
        in_specs=(P("rep", None, None),) * 2 + (P("pp", None, None),) * 3,
        out_specs=(P(("rep", "pp"), None, None),) * 3,
        check_vma=False,
    )
```

profile of v0, /device:TPU:17, one launch (start us, length us, event | category | flops | bytes accessed | tf_op | source)
XLA Modules:
  0.0 1141.8 jit_solution(8275098610988378879)
XLA Ops:
  6.3 5.5 fusion.812
  15.6 6.1 collective-permute-done
  26.0 5.3 fusion.809
  31.3 4.4 collective-permute-start.1
  35.7 6.1 collective-permute-done.1
  46.1 5.4 fusion.806
  51.5 4.4 collective-permute-start.2
  55.9 6.1 collective-permute-done.2
  66.3 6.2 fusion.803
  72.4 4.6 collective-permute-start.3
  77.0 5.9 collective-permute-done.3
  87.2 6.2 fusion.800
  97.8 6.1 collective-permute-done.4
  108.9 6.3 fusion.797
  119.7 6.1 collective-permute-done.5
  130.8 6.3 fusion.794
  141.6 6.1 collective-permute-done.6
  152.7 6.3 fusion.791
  159.1 4.8 collective-permute-start.7
  163.9 5.7 collective-permute-done.7
  174.7 6.3 fusion.788
  185.4 6.1 collective-permute-done.8
  196.5 6.3 fusion.785
  207.3 6.0 collective-permute-done.9
  218.6 6.3 fusion.782
  225.0 4.7 collective-permute-start.10
  244.2 6.4 fusion.779
  263.8 6.4 fusion.776
  270.2 4.4 collective-permute-start.12
  285.0 6.2 fusion.773
  291.2 4.6 collective-permute-start.13
  306.0 6.3 fusion.770
  327.8 6.4 fusion.767
  349.8 6.4 fusion.764
  356.3 4.8 collective-permute-start.16
  372.0 6.4 fusion.761
  393.0 6.2 fusion.758
  399.2 4.4 collective-permute-start.18
  414.0 6.2 fusion.755
  420.2 4.6 collective-permute-start.19
  435.0 6.2 fusion.752
  456.0 6.1 fusion.749
  462.1 4.6 collective-permute-start.21
  495.7 6.3 fusion.1025
  1038.1 6.1 collective-permute-done.42
  1076.6 21.0 %fusion.393 = bf16[1,512,1792]{2,1,0:T(8,128)(2,1)} fusion(pred[]{:T(512)S(6)} %and.184, bf16[512,1792]{1,0:T(8,128)(2,1)} %convolution_convert_fusion.23, pred[]{:T(512)S(6)} %and.183, bf16[512,1792]{1,0:T(8,128)(2,1)} %convolution_convert_fusion.24, pred[]{:T(512)S(6)} %and.182, bf16[512,1792]{1,0:T(8,128)(2,1)} %convolution_convert_fusion.25, ...), kind=kOutput, calls=%fused_computation.620 | convolution fusion | flops 1010040832 | bytes 48236572 | tf_op jit(solution)/shard_map/transpose(jvp())/dot_general | solution.py:22
  1097.7 22.4 %fusion.392 = bf16[1,512,1792]{2,1,0:T(8,128)(2,1)} fusion(pred[]{:T(512)S(6)} %and.184, bf16[512,1792]{1,0:T(8,128)(2,1)} %convolution_convert_fusion.46, pred[]{:T(512)S(6)} %and.183, bf16[512,1792]{1,0:T(8,128)(2,1)} %convolution_convert_fusion.48, pred[]{:T(512)S(6)} %and.182, bf16[512,1792]{1,0:T(8,128)(2,1)} %convolution_convert_fusion.50, ...), kind=kOutput, calls=%fused_computation.619 | convolution fusion | flops 1014628352 | bytes 51906588 | tf_op jit(solution)/shard_map/transpose(jvp())/dot_general | solution.py:21
  1120.0 21.4 %fusion.394 = bf16[1,1792,512]{2,1,0:T(8,128)(2,1)} fusion(pred[]{:T(512)S(6)} %and.184, bf16[1792,512]{1,0:T(8,128)(2,1)} %convolution_convert_fusion.1, pred[]{:T(512)S(6)} %and.183, bf16[1792,512]{1,0:T(8,128)(2,1)} %convolution_convert_fusion.2, pred[]{:T(512)S(6)} %and.182, bf16[1792,512]{1,0:T(8,128)(2,1)} %convolution_convert_fusion.3, ...), kind=kOutput, calls=%fused_computation.621 | convolution fusion | flops 1009516544 | bytes 50593816 | tf_op jit(solution)/shard_map/transpose(jvp())/dot_general | solution.py:10
  (676 shorter events, 814.3 us)
Async XLA Ops:
  11.8 9.9 collective-permute-start
  31.3 10.5 collective-permute-start.1
  51.5 10.5 collective-permute-start.2
  72.4 10.5 collective-permute-start.3
  93.4 10.5 collective-permute-start.4
  115.3 10.5 collective-permute-start.5
  137.2 10.5 collective-permute-start.6
  159.1 10.5 collective-permute-start.7
  181.0 10.5 collective-permute-start.8
  202.9 10.5 collective-permute-start.9
  225.0 14.2 %collective-permute-start.10 = (bf16[512,512]{1,0:T(8,128)(2,1)}, bf16[512,512]{1,0:T(8,128)(2,1)S(1)}, u32[]{:S(2)}, u32[]{:S(2)}) collective-permute-start(bf16[512,512]{1,0:T(8,128)(2,1)} %fusion.782), channel_id=1, source_target_pairs={{0,1},{1,2},{2,3},{3,4},{4,5},{5,6},{6,7},{8,9},{9,10},{10,11},{11... | collective-permute-start | bytes 1572872 | tf_op jit(solution)/shard_map/ppermute | solution.py:47
  250.6 8.0 collective-permute-start.11
  270.2 10.5 collective-permute-start.12
  291.2 10.5 collective-permute-start.13
  312.3 10.5 collective-permute-start.14
  334.2 10.5 collective-permute-start.15
  356.3 10.7 collective-permute-start.16
  378.4 10.3 collective-permute-start.17
  399.2 10.5 collective-permute-start.18
  420.2 10.5 collective-permute-start.19
  441.2 10.5 collective-permute-start.20
  462.1 10.5 collective-permute-start.21
  502.1 65.9 %copy-start.78 = (f32[512]{0:T(512)}, f32[512]{0:T(512)S(1)}, u32[]{:S(2)}) copy-start(f32[512]{0:T(512)S(1)} %get-tuple-element.7) | copy-start | bytes 6148
  502.2 61.6 %copy-start.46 = (f32[512]{0:T(512)}, f32[512]{0:T(512)S(1)}, u32[]{:S(2)}) copy-start(f32[512]{0:T(512)S(1)} %fusion.1428) | copy-start | bytes 6148
  502.2 57.6 %copy-start.50 = (f32[512]{0:T(512)}, f32[512]{0:T(512)S(1)}, u32[]{:S(2)}) copy-start(f32[512]{0:T(512)S(1)} %fusion.1427) | copy-start | bytes 6148
  502.2 53.5 %copy-start.52 = (f32[512]{0:T(512)}, f32[512]{0:T(512)S(1)}, u32[]{:S(2)}) copy-start(f32[512]{0:T(512)S(1)} %fusion.1426) | copy-start | bytes 6148
  503.9 68.3 %collective-permute-start.22 = (bf16[512,512]{1,0:T(8,128)(2,1)S(1)}, bf16[512,512]{1,0:T(8,128)(2,1)S(1)}, u32[]{:S(2)}, u32[]{:S(2)}) collective-permute-start(bf16[512,512]{1,0:T(8,128)(2,1)S(1)} %fusion.1146), channel_id=1, source_target_pairs={{1,0},{2,1},{3,2},{4,3},{5,4},{6,5},{7,6},{9,8},{10,9},{11,10},{12... | collective-permute-start | bytes 1572872 | tf_op jit(solution)/shard_map/ppermute | solution.py:57
  592.5 10.7 collective-permute-start.23
  615.4 10.5 collective-permute-start.24
  637.9 10.5 collective-permute-start.25
  660.5 10.5 collective-permute-start.26
  683.7 10.5 collective-permute-start.27
  706.9 10.5 collective-permute-start.28
  729.7 10.5 collective-permute-start.29
  752.7 10.5 collective-permute-start.30
  775.4 10.5 collective-permute-start.31
  798.1 10.5 collective-permute-start.32
  820.9 10.5 collective-permute-start.33
  843.8 10.5 collective-permute-start.34
  866.5 10.5 collective-permute-start.35
  889.3 10.5 collective-permute-start.36
  912.0 10.5 collective-permute-start.37
  934.8 10.5 collective-permute-start.38
  957.6 10.5 collective-permute-start.39
  980.4 10.5 collective-permute-start.40
  1003.1 10.5 collective-permute-start.41
  1033.7 10.5 collective-permute-start.42
  1060.7 13.5 %collective-permute-start.43 = (bf16[512,512]{1,0:T(8,128)(2,1)S(1)}, bf16[512,512]{1,0:T(8,128)(2,1)S(1)}, u32[]{:S(2)}, u32[]{:S(2)}) collective-permute-start(bf16[512,512]{1,0:T(8,128)(2,1)S(1)} %fusion.1125), channel_id=1, source_target_pairs={{1,0},{2,1},{3,2},{4,3},{5,4},{6,5},{7,6},{9,8},{10,9},{11,10},{12... | collective-permute-start | bytes 1572872 | tf_op jit(solution)/shard_map/ppermute | solution.py:57
  (111 other events, 834.0 us)
where the time goes:
time: 1160 us; the launch traced here: 1140 us
  matrix products  763 us (66%)
  starting transfers between devices  147 us (13%)
  other arithmetic  96.3 us (8%)
  waiting for transfers between devices  85.6 us (7%)
  local copies, waits for them, and re-layouts  46.6 us (4%)
    dot_general x90, matrix products, layer(): gate = jnp.dot(a, w['w_gate'], preferred_element_type=jnp.float32)  266 us
    dot_general x68, matrix products, layer(): up = jnp.dot(a, w['w_up'], preferred_element_type=jnp.float32)  250 us
    dot_general x68, matrix products, matmul(): jnp.dot(a, w, preferred_element_type=jnp.float32).astype(jnp.bfloat16)  246 us
    ppermute x22, starting transfers between devices, step(): came = lax.ppermute(stage(weights, h), 'pp', onward)  95.4 us
    ppermute x22, waiting for transfers between devices, step(): came = lax.ppermute(stage(weights, h), 'pp', onward)  65.7 us
    ppermute x22, starting transfers between devices, step(): came = lax.ppermute(by_h, 'pp', back_again)  51.4 us
    dynamic_update_slice x23, other arithmetic, step(): lax.dynamic_update_index_in_dim(kept, jnp.where(at_work, h, was), number, 0)  33.3 us
    dynamic_slice x22, local copies, waits for them, and re-layouts, step(): was = lax.dynamic_index_in_dim(kept, number, 0, keepdims=False)  30.9 us
  transfers between devices with their start and end apart: 44, of which 38 were waited for; matrix products, arithmetic and copies ran while one was open for 25% of the time, Pallas kernels for 0%

commit v1 on v0

v1 whole, which is shorter than its diff:
```python
import functools

import jax
import jax.numpy as jnp
from jax import lax
from jax.experimental import pallas as pl
from jax.experimental.pallas import tpu as pltpu
from jax.sharding import PartitionSpec as P

MESH = pl.DeviceIdType.MESH
BF, F32 = jnp.bfloat16, jnp.float32
STAGES = 8
AHEAD = (24, 20, 17, 14, 10, 7, 4, 0)
LATE = 1
RING = 4


def dot(a, b):
    return jnp.dot(a, b, preferred_element_type=F32)


def dot_t(a, b):
    return lax.dot_general(a, b, (((1,), (1,)), ((), ())), preferred_element_type=F32)


def norm_of(h):
    wide = h.astype(F32)
    scale = lax.rsqrt(jnp.mean(wide * wide, -1, keepdims=True) + 1e-6)
    return wide, scale, (wide * scale).astype(BF)


def kernel(
    chunk, tile, x_ref, dy_ref, wg_ref, wu_ref, wd_ref, og_ref, ou_ref, od_ref, gu_hbm,
    wg, wu, wd, acc, hst, dst, gu, hid, wst, a_t, dy_t, fout, bout,
    wsem, frecv, brecv, fsend, bsend, gout, gin, osem,
):
    s = lax.axis_index("pp")
    last = STAGES - 1
    micro, tokens, d = x_ref.shape
    ff = wg.shape[1]
    per = tokens // chunk
    chunks = micro * per
    tiles = ff // tile
    ahead = sum(jnp.where(s == i, n, 0) for i, n in enumerate(AHEAD))

    def part(ref, c):
        return ref.at[c // per, pl.ds(lax.rem(c, per) * chunk, chunk)]

    def got_f(c):
        return pltpu.make_async_copy(part(x_ref, c), hst.at[c], frecv.at[c])

    def got_b(c):
        return pltpu.make_async_copy(part(dy_ref, c), dst.at[c], brecv.at[c])

    def send_f(c):
        slot = lax.rem(c, RING)
        return pltpu.make_async_remote_copy(
            fout.at[slot], hst.at[c], fsend.at[slot], frecv.at[c], device_id={"pp": s + 1}, device_id_type=MESH
        )

    def send_b(c):
        slot = lax.rem(c, RING)
        return pltpu.make_async_remote_copy(
            bout.at[slot], dst.at[c], bsend.at[slot], brecv.at[c], device_id={"pp": s - 1}, device_id_type=MESH
        )

    def put_gu(c):
        slot = lax.rem(c, 2)
        return pltpu.make_async_copy(gu.at[slot], gu_hbm.at[c], gout.at[slot])

    def get_gu(c):
        slot = lax.rem(c, 2)
        return pltpu.make_async_copy(gu_hbm.at[c], gu.at[slot + 2], gin.at[slot])

    loads = [
        pltpu.make_async_copy(src.at[0], dst_, wsem.at[i])
        for i, (src, dst_) in enumerate(((wg_ref, wg), (wu_ref, wu), (wd_ref, wd)))
    ]

    @pl.when(s == 0)
    def _():
        got_f(0).start()

    for copy in loads:
        copy.start()

    barrier = pltpu.get_barrier_semaphore()
    for by in (1, STAGES - 1):
        pl.semaphore_signal(barrier, inc=1, device_id={"pp": lax.rem(s + by, STAGES)}, device_id_type=MESH)

    @pl.when(s == 0)
    def _():
        @pl.loop(1, chunks)
        def _(c):
            got_f(c).start()

    @pl.when(s == last)
    def _():
        @pl.loop(0, chunks)
        def _(c):
            got_b(c).start()

    def clear():
        @pl.loop(0, 3 * (d // 32))
        def _(i):
            j, r = i // (d // 32), lax.rem(i, d // 32)
            acc[j, pl.ds(r * 32, 32), :] = jnp.zeros((32, ff), F32)

    pl.when(s > 0)(clear)
    pl.semaphore_wait(barrier, 2)
    for copy in loads:
        copy.wait()

    def gate_up(c, slot, keep_hid):
        _, _, a = norm_of(hst[c])
        for n in range(tiles):
            cols = slice(n * tile, (n + 1) * tile)
            g, u = dot(a, wg[:, cols]), dot(a, wu[:, cols])
            gu[slot, 0, :, cols] = g
            gu[slot, 1, :, cols] = u
            if keep_hid:
                hid[:, cols] = (g * jax.nn.sigmoid(g) * u).astype(BF)

    def forward(c):
        slot = lax.rem(c, 2)
        got_f(c).wait()

        @pl.when(s == last)
        def _():
            gate_up(c, slot, False)

        @pl.when(s < last)
        def _():
            out = lax.rem(c, RING)

            @pl.when(c >= RING)
            def _():
                send_f(c - RING).wait_send()

            gate_up(c, slot, True)
            y = dot(hid[...], wd[...]).astype(BF)
            fout[out] = (hst[c].astype(F32) + y.astype(F32)).astype(BF)
            send_f(c).start()
            put_gu(c).start()

    def inner(c, slot, w_slot, rows):
        dy = dst[c]
        dy_t[w_slot, :, rows] = dy.T
        for n in range(tiles):
            cols = slice(n * tile, (n + 1) * tile)
            dh = dot_t(dy, wd[cols, :]).astype(BF).astype(F32)
            g, u = gu[slot, 0, :, cols], gu[slot, 1, :, cols]
            sig = jax.nn.sigmoid(g)
            silu = g * sig
            wst[w_slot, 2, rows, cols] = (silu * u).astype(BF)
            wst[w_slot, 1, rows, cols] = (dh * silu).astype(BF)
            wst[w_slot, 0, rows, cols] = (dh * u * (sig + silu * (1.0 - sig))).astype(BF)

    def backward(c):
        m = c // per
        w_slot = lax.rem(m, LATE + 1)
        slot = jnp.where(s == last, lax.rem(c, 2), lax.rem(c, 2) + 2)
        got_b(c).wait()

        @pl.when(s < last)
        def _():
            get_gu(c).wait()

        for half in range(per):
            rows = slice(half * chunk, (half + 1) * chunk)

            @pl.when((s == 0) & (lax.rem(c, per) == half))
            def _():
                a_t[w_slot, :, rows] = norm_of(hst[c])[2].T
                inner(c, slot, w_slot, rows)

            @pl.when((s > 0) & (lax.rem(c, per) == half))
            def _():
                out = lax.rem(c, RING)

                @pl.when(c >= RING)
                def _():
                    send_b(c - RING).wait_send()

                wide, scale, a = norm_of(hst[c])
                a_t[w_slot, :, rows] = a.T
                inner(c, slot, w_slot, rows)
                da = dot_t(wst[w_slot, 0, rows, :], wg[...]).astype(BF).astype(F32)
                da = (da + dot_t(wst[w_slot, 1, rows, :], wu[...]).astype(BF).astype(F32)).astype(BF).astype(F32)
                inner_sum = jnp.sum(da * wide, -1, keepdims=True) * (1.0 / d)
                dwide = scale * da - wide * (scale * scale * scale * inner_sum)
                bout[out] = (dst[c].astype(F32) + dwide.astype(BF).astype(F32)).astype(BF)
                send_b(c).start()

    def weights(m):
        slot = lax.rem(m, LATE + 1)
        for j in range(3):
            for n in range(tiles):
                cols = slice(n * tile, (n + 1) * tile)
                lhs = dy_t[slot] if j == 2 else a_t[slot]
                term = dot(lhs, wst[slot, j, :, cols]).astype(BF).astype(F32)
                acc[j, :, cols] = acc[j, :, cols] + term

    @pl.loop(0, chunks + max(AHEAD) + per * LATE)
    def _(t):
        @pl.when((s < last) & (t >= 2) & (t < chunks + 2))
        def _():
            put_gu(t - 2).wait()

        @pl.when(t < chunks)
        def _():
            forward(t)

        soon = t - ahead + 1

        @pl.when((s < last) & (soon >= 0) & (soon < chunks))
        def _():
            get_gu(soon).start()

        back = t - ahead
        pl.when((s == 0) & (back == 0))(clear)

        @pl.when((back >= 0) & (back < chunks))
        def _():
            backward(back)

        m = (back + 1) // per - 1 - LATE

        @pl.when((lax.rem(back + 1, per) == 0) & (back + 1 > per * LATE) & (m < micro))
        def _():
            weights(m)

    @pl.when(s < last)
    def _():
        @pl.loop(chunks - RING, chunks)
        def _(c):
            send_f(c).wait_send()

    @pl.when(s > 0)
    def _():
        @pl.loop(chunks - RING, chunks)
        def _(c):
            send_b(c).wait_send()

    copies = []
    for j, ref in enumerate((og_ref, ou_ref, od_ref)):
        for n in range(tiles):
            cols = slice(n * tile, (n + 1) * tile)
            wst[0, j, :, cols] = acc[j, :, cols].astype(BF)
        copies.append(pltpu.make_async_copy(wst.at[0, j], ref.at[0], osem.at[j]))
        copies[-1].start()
    for copy in copies:
        copy.wait()


def solution(mesh):
    def step(x, dy, w_gate, w_up, w_down):
        micro, tokens, d = x.shape
        ff = w_gate.shape[2]
        chunk, tile = tokens // 2, 256
        chunks = 2 * micro
        any_, vmem = pl.BlockSpec(memory_space=pl.ANY), pltpu.VMEM
        dma = pltpu.SemaphoreType.DMA
        flat = jax.ShapeDtypeStruct((1, d, ff), BF)
        by_gate, by_up, by_down, _ = pl.pallas_call(
            functools.partial(kernel, chunk, tile),
            name="stages",
            out_shape=(flat, flat, flat, jax.ShapeDtypeStruct((chunks, 2, chunk, ff), F32)),
            in_specs=[any_] * 5,
            out_specs=(any_,) * 4,
            scratch_shapes=[
                vmem((d, ff), BF),
                vmem((d, ff), BF),
                vmem((ff, d), BF),
                vmem((3, d, ff), F32),
                vmem((chunks, chunk, d), BF),
                vmem((chunks, chunk, d), BF),
                vmem((4, 2, chunk, ff), F32),
                vmem((chunk, ff), BF),
                vmem((LATE + 1, 3, tokens, ff), BF),
                vmem((LATE + 1, d, tokens), BF),
                vmem((LATE + 1, d, tokens), BF),
                vmem((RING, chunk, d), BF),
                vmem((RING, chunk, d), BF),
                dma((3,)),
                dma((chunks,)),
                dma((chunks,)),
                dma((RING,)),
                dma((RING,)),
                dma((2,)),
                dma((2,)),
                dma((3,)),
            ],
            compiler_params=pltpu.CompilerParams(
                collective_id=0, has_side_effects=True, vmem_limit_bytes=67043328
            ),
        )(x, dy, w_gate, w_up, w_down)
        return by_gate, by_up, jnp.swapaxes(by_down, 1, 2)

    return jax.shard_map(
        step,
        mesh=mesh,
        in_specs=(P("rep", None, None),) * 2 + (P("pp", None, None),) * 3,
        out_specs=(P(("rep", "pp"), None, None),) * 3,
        check_vma=False,
    )
```

time: 1160 us -> 257 us (0.22)
  the two profiles are of different devices: /device:TPU:17 before, /device:TPU:0 now
where the time goes in v1:
time: 257 us; the launch traced here: 256 us
  Pallas kernels  248 us (96%)
  local copies, waits for them, and re-layouts  7.36 us (3%)
    pallas_call x1, Pallas kernels, step(): pl.pallas_call(functools.partial(kernel, chunk, tile), name='stages', out...  248 us
    unnamed x7, local copies, waits for them, and re-layouts  7.36 us

profile of v1, /device:TPU:0, one launch (start us, length us, event | category | flops | bytes accessed | tf_op | source)
XLA Modules:
  0.0 256.3 jit_solution(15141561188329398498)
XLA Ops:
  0.6 248.3 %stages.1 = (bf16[1,512,1792]{2,1,0:T(8,128)(2,1)}, bf16[1,512,1792]{2,1,0:T(8,128)(2,1)}, bf16[1,512,1792]{2,1,0:T(8,128)(2,1)}, f32[32,2,256,1792]{3,2,1,0:T(8,128)}) custom-call(bf16[16,512,512]{2,1,0:T(8,128)(2,1)} %x_ref.1, bf16[16,512,512]{2,1,0:T(8,128)(2,1)} %dy_ref.1, bf16[1,512,1792]{2,1,0:T(8,128)(2,1)} %wg_ref.1, bf16[1,512,1792]{2,1,0:T(8,128)(2,1)} %wu_ref.1, ...), custom_call_target="tpu_custom_call" | custom-call | tf_op jit(solution)/shard_map/stages/pallas_call | solution.py:265
  249.0 0.0 copy-start.1
  249.0 4.0 %copy.8 = bf16[1,1792,512]{2,1,0:T(8,128)(2,1)} copy(bf16[1,1792,512]{1,2,0:T(8,128)(2,1)} %bitcast.1) | data formatting | bytes 3670016
  252.9 0.0 copy-done.1
  252.9 0.0 copy-start
  253.0 1.2 copy.11
  254.2 0.9 copy-done
  255.1 1.2 copy.12
Async XLA Ops:
  249.0 4.0 %copy-start.1 = (bf16[1,512,1792]{2,1,0:T(8,128)(2,1)S(1)}, bf16[1,512,1792]{2,1,0:T(8,128)(2,1)}, u32[]{:S(2)}) copy-start(bf16[1,512,1792]{2,1,0:T(8,128)(2,1)} %get-tuple-element.15) | copy-start | bytes 5505028
  252.9 2.2 copy-start

commit v2 on v1

v2 whole, which is shorter than its diff:
```python
import functools

import jax
import jax.numpy as jnp
from jax import lax
from jax.experimental import pallas as pl
from jax.experimental.pallas import tpu as pltpu
from jax.sharding import PartitionSpec as P

MESH = pl.DeviceIdType.MESH
BF, F32 = jnp.bfloat16, jnp.float32
STAGES = 8
LANES = 128
AHEAD = (31, 27, 19, 16, 11, 8, 3, 0)
NEAR = 4
LATE = (2, 2, 4, 5, 7, 8, 11, 12)
RING = 4


def dot(a, b):
    return jnp.dot(a, b, preferred_element_type=F32)


def dot_t(a, b):
    return lax.dot_general(a, b, (((1,), (1,)), ((), ())), preferred_element_type=F32)


def kernel(
    chunk, tile, x_ref, dy_ref, wg_ref, wu_ref, wd_ref, og_ref, ou_ref, od_ref, gu_hbm, w_hbm,
    wg, wu, wd, acc, hst, dst, gu, hid, dgu, win, cur, abuf, fbuf, sbuf, fout, bout,
    wsem, frecv, brecv, fsend, bsend, gout, gin, hout, dout, wsin, osem,
):
    s = lax.axis_index("pp")
    last = STAGES - 1
    micro, tokens, d = x_ref.shape
    ff = wg.shape[1]
    per = tokens // chunk
    chunks = micro * per
    tiles = ff // tile
    ahead = sum(jnp.where(s == i, n, 0) for i, n in enumerate(AHEAD))
    late = sum(jnp.where(s == i, n, 0) for i, n in enumerate(LATE))
    near = ahead < NEAR
    strip = min(chunk, 64)
    strips = [slice(r, r + strip) for r in range(0, chunk, strip)]
    blocks = d // chunk

    def part(ref, c):
        return ref.at[c // per, pl.ds(lax.rem(c, per) * chunk, chunk)]

    def got_f(c):
        return pltpu.make_async_copy(part(x_ref, c), hst.at[c], frecv.at[c])

    def got_b(c):
        return pltpu.make_async_copy(part(dy_ref, c), dst.at[c], brecv.at[c])

    def send_f(c):
        slot = lax.rem(c, RING)
        return pltpu.make_async_remote_copy(
            fout.at[slot], hst.at[c], fsend.at[slot], frecv.at[c], device_id={"pp": s + 1}, device_id_type=MESH
        )

    def send_b(c):
        slot = lax.rem(c, RING)
        return pltpu.make_async_remote_copy(
            bout.at[slot], dst.at[c], bsend.at[slot], brecv.at[c], device_id={"pp": s - 1}, device_id_type=MESH
        )

    def put_gu(c):
        slot = lax.rem(c, 2)
        return pltpu.make_async_copy(gu.at[slot], gu_hbm.at[c], gout.at[slot])

    def get_gu(c):
        slot = lax.rem(c, 2)
        return pltpu.make_async_copy(gu_hbm.at[c], gu.at[slot + 2], gin.at[slot])

    def put_hid(c):
        slot = lax.rem(c, 2)
        to = w_hbm.at[c // per, 2, pl.ds(lax.rem(c, per) * chunk, chunk)]
        return pltpu.make_async_copy(hid.at[slot], to, hout.at[slot])

    def put_dgu(c):
        slot = lax.rem(c, 2)
        to = w_hbm.at[c // per, pl.ds(0, 2), pl.ds(lax.rem(c, per) * chunk, chunk)]
        return pltpu.make_async_copy(dgu.at[slot], to, dout.at[slot])

    def get_w(m):
        return pltpu.make_async_copy(w_hbm.at[m], win, wsin)

    loads = [
        pltpu.make_async_copy(src.at[0], dst_, wsem.at[i])
        for i, (src, dst_) in enumerate(((wg_ref, wg), (wu_ref, wu), (wd_ref, wd)))
    ]

    @pl.when(s == 0)
    def _():
        got_f(0).start()

    for copy in loads:
        copy.start()

    barrier = pltpu.get_barrier_semaphore()
    for by in (1, STAGES - 1):
        pl.semaphore_signal(barrier, inc=1, device_id={"pp": lax.rem(s + by, STAGES)}, device_id_type=MESH)

    @pl.when(s == 0)
    def _():
        @pl.loop(1, chunks)
        def _(c):
            got_f(c).start()

    @pl.when(s == last)
    def _():
        @pl.loop(0, chunks)
        def _(c):
            got_b(c).start()

    def clear():
        @pl.loop(0, 3 * (d // 32))
        def _(i):
            j, r = i // (d // 32), lax.rem(i, d // 32)
            acc[j, pl.ds(r * 32, 32), :] = jnp.zeros((32, ff), F32)

    pl.when(s > 0)(clear)
    pl.semaphore_wait(barrier, 2)
    for copy in loads:
        copy.wait()

    def norm(h, to, sbuf=None):
        for rows in strips:
            wide = h[rows, :].astype(F32)
            scale = lax.rsqrt(jnp.mean(wide * wide, -1, keepdims=True) + 1e-6)
            if sbuf is not None:
                sbuf[rows, :] = jnp.broadcast_to(scale, (strip, LANES))
            to[rows, :] = (wide * scale).astype(BF)

    def gate_up(c, slot):
        norm(hst[c], fbuf)
        h_slot = lax.rem(c, 2)
        a = fbuf[...]
        for n in range(tiles):
            cols = slice(n * tile, (n + 1) * tile)
            g, u = dot(a, wg[:, cols]), dot(a, wu[:, cols])
            sig = jax.nn.sigmoid(g)
            silu = g * sig
            gu[slot, 0, :, cols] = u * (sig + silu * (1.0 - sig))
            gu[slot, 1, :, cols] = silu
            hid[h_slot, :, cols] = (silu * u).astype(BF)

    def down(c, out):
        y = dot(hid[lax.rem(c, 2)], wd[...]).astype(BF)
        fout[out] = (hst[c].astype(F32) + y.astype(F32)).astype(BF)

    def forward(c):
        slot = jnp.where(near, lax.rem(c, 4), lax.rem(c, 2))
        got_f(c).wait()

        @pl.when(s == last)
        def _():
            gate_up(c, slot)

        @pl.when(s < last)
        def _():
            out = lax.rem(c, RING)

            @pl.when(c >= RING)
            def _():
                send_f(c - RING).wait_send()

            gate_up(c, slot)
            down(c, out)
            send_f(c).start()

        put_hid(c).start()

        @pl.when(jnp.logical_not(near))
        def _():
            put_gu(c).start()

    def turn(ref, c, value):
        t = value.T
        for i in range(blocks):
            ref[c, :, i * chunk : (i + 1) * chunk] = t[i * chunk : (i + 1) * chunk, :]

    def inner(c, slot, to):
        dy = cur[1]
        for n in range(tiles):
            cols = slice(n * tile, (n + 1) * tile)
            dh = dot_t(dy, wd[cols, :]).astype(BF).astype(F32)
            dgu[to, 0, :, cols] = (dh * gu[slot, 0, :, cols]).astype(BF)
            dgu[to, 1, :, cols] = (dh * gu[slot, 1, :, cols]).astype(BF)

    def back_to_hidden(c, slot, to):
        cur[0] = hst[c]
        cur[1] = dst[c]
        norm(cur[0], abuf, sbuf)
        inner(c, slot, to)
        turn(dst, c, cur[1])
        turn(hst, c, abuf[...])

    def back_to_states(to, out):
        da0 = dot_t(dgu[to, 0], wg[...]).astype(BF).astype(F32)
        da1 = dot_t(dgu[to, 1], wu[...]).astype(BF).astype(F32)
        for rows in strips:
            da = (da0[rows, :] + da1[rows, :]).astype(BF).astype(F32)
            wide = cur[0, rows, :].astype(F32)
            scale = jnp.concatenate([sbuf[rows, :]] * (d // LANES), axis=1)
            inner_sum = jnp.sum(da * wide, -1, keepdims=True) * (1.0 / d)
            dwide = scale * da - wide * (scale * scale * scale * inner_sum)
            bout[out, rows, :] = (cur[1, rows, :].astype(F32) + dwide.astype(BF).astype(F32)).astype(BF)

    def both_ways(c, b):
        out_f, out_b, to = lax.rem(c, RING), lax.rem(b, RING), lax.rem(b, 2)
        f_slot = jnp.where(near, lax.rem(c, 4), lax.rem(c, 2))
        b_slot = jnp.where(near, lax.rem(b, 4), lax.rem(b, 2) + 2)
        got_f(c).wait()
        got_b(b).wait()

        @pl.when(jnp.logical_not(near))
        def _():
            get_gu(b).wait()

        @pl.when(c >= RING)
        def _():
            send_f(c - RING).wait_send()

        @pl.when(b >= RING)
        def _():
            send_b(b - RING).wait_send()

        back_to_hidden(b, b_slot, to)
        gate_up(c, f_slot)
        back_to_states(to, out_b)
        down(c, out_f)
        send_b(b).start()
        send_f(c).start()
        put_hid(c).start()
        put_dgu(b).start()

        @pl.when(jnp.logical_not(near))
        def _():
            put_gu(c).start()

    def backward(c):
        to = lax.rem(c, 2)
        slot = jnp.where(near, lax.rem(c, 4), lax.rem(c, 2) + 2)
        got_b(c).wait()

        @pl.when(jnp.logical_not(near))
        def _():
            get_gu(c).wait()

        @pl.when(s == 0)
        def _():
            cur[1] = dst[c]
            norm(hst[c], abuf)
            inner(c, slot, to)
            turn(dst, c, cur[1])
            turn(hst, c, abuf[...])

        @pl.when(s > 0)
        def _():
            out = lax.rem(c, RING)

            @pl.when(c >= RING)
            def _():
                send_b(c - RING).wait_send()

            back_to_hidden(c, slot, to)
            back_to_states(to, out)
            send_b(c).start()

        put_dgu(c).start()

    def weights(m):
        get_w(m).wait()
        for j, ref in ((2, dst), (0, hst), (1, hst)):
            lhs = [
                jnp.concatenate([ref[m * per + k, :, i * chunk : (i + 1) * chunk] for i in range(blocks)], axis=0)
                for k in range(per)
            ]
            for n in range(tiles):
                cols = slice(n * tile, (n + 1) * tile)
                term = sum(dot(lhs[k], win[j, k * chunk : (k + 1) * chunk, cols]) for k in range(per))
                acc[j, :, cols] = acc[j, :, cols] + term.astype(BF).astype(F32)

    @pl.loop(0, chunks + max(n + per * l for n, l in zip(AHEAD, LATE)))
    def _(t):
        @pl.when((t >= 2) & (t < chunks + 2))
        def _():
            put_hid(t - 2).wait()

            @pl.when(jnp.logical_not(near))
            def _():
                put_gu(t - 2).wait()

        soon, back = t - ahead + 2, t - ahead

        @pl.when((back >= 2) & (back < chunks + 2))
        def _():
            put_dgu(back - 2).wait()

        m = (back + 1) // per - 1 - late
        due = (lax.rem(back + 1, per) == 0) & (back + 1 > per * late) & (m < micro)

        early = back // per - late

        @pl.when((lax.rem(back, per) == 0) & (back >= per * late) & (early < micro))
        def _():
            get_w(early).start()

        both = (s > 0) & (s < last) & (t < chunks) & (back >= 0)
        pl.when(both)(lambda: both_ways(t, back))
        alone = jnp.logical_not(both)
        pl.when(alone & (t < chunks))(lambda: forward(t))
        pl.when((s == 0) & (back == 0))(clear)
        pl.when(alone & (back >= 0) & (back < chunks))(lambda: backward(back))

        @pl.when(jnp.logical_not(near) & (soon >= 0) & (soon < chunks))
        def _():
            get_gu(soon).start()

        @pl.when(due)
        def _():
            weights(m)

    @pl.when(s < last)
    def _():
        @pl.loop(chunks - RING, chunks)
        def _(c):
            send_f(c).wait_send()

    @pl.when(s > 0)
    def _():
        @pl.loop(chunks - RING, chunks)
        def _(c):
            send_b(c).wait_send()

    copies = []
    for j, ref in enumerate((og_ref, ou_ref, od_ref)):
        for n in range(tiles):
            cols = slice(n * tile, (n + 1) * tile)
            win[j, :, cols] = acc[j, :, cols].astype(BF)
        copies.append(pltpu.make_async_copy(win.at[j], ref.at[0], osem.at[j]))
        copies[-1].start()
    for copy in copies:
        copy.wait()


def solution(mesh):
    def step(x, dy, w_gate, w_up, w_down):
        micro, tokens, d = x.shape
        ff = w_gate.shape[2]
        chunk, tile = tokens // 2, 256
        chunks = 2 * micro
        any_, vmem = pl.BlockSpec(memory_space=pl.ANY), pltpu.VMEM
        dma = pltpu.SemaphoreType.DMA
        flat = jax.ShapeDtypeStruct((1, d, ff), BF)
        by_gate, by_up, by_down, _, _ = pl.pallas_call(
            functools.partial(kernel, chunk, tile),
            name="stages",
            out_shape=(
                flat,
                flat,
                flat,
                jax.ShapeDtypeStruct((chunks, 2, chunk, ff), F32),
                jax.ShapeDtypeStruct((micro, 3, tokens, ff), BF),
            ),
            in_specs=[any_] * 5,
            out_specs=(any_,) * 5,
            scratch_shapes=[
                vmem((d, ff), BF),
                vmem((d, ff), BF),
                vmem((ff, d), BF),
                vmem((3, d, ff), F32),
                vmem((chunks, chunk, d), BF),
                vmem((chunks, chunk, d), BF),
                vmem((4, 2, chunk, ff), F32),
                vmem((2, chunk, ff), BF),
                vmem((2, 2, chunk, ff), BF),
                vmem((3, tokens, ff), BF),
                vmem((2, chunk, d), BF),
                vmem((chunk, d), BF),
                vmem((chunk, d), BF),
                vmem((chunk, LANES), F32),
                vmem((RING, chunk, d), BF),
                vmem((RING, chunk, d), BF),
                dma((3,)),
                dma((chunks,)),
                dma((chunks,)),
                dma((RING,)),
                dma((RING,)),
                dma((2,)),
                dma((2,)),
                dma((2,)),
                dma((2,)),
                dma,
                dma((3,)),
            ],
            compiler_params=pltpu.CompilerParams(
                collective_id=0, has_side_effects=True, vmem_limit_bytes=67043328
            ),
        )(x, dy, w_gate, w_up, w_down)
        return by_gate, by_up, jnp.swapaxes(by_down, 1, 2)

    return jax.shard_map(
        step,
        mesh=mesh,
        in_specs=(P("rep", None, None),) * 2 + (P("pp", None, None),) * 3,
        out_specs=(P(("rep", "pp"), None, None),) * 3,
        check_vma=False,
    )
```

time: 257 us -> 245 us (0.953)
  the two profiles are of different devices: /device:TPU:0 before, /device:TPU:27 now
where the time goes in v2:
time: 245 us; the launch traced here: 244 us
  Pallas kernels  236 us (96%)
  local copies, waits for them, and re-layouts  7.36 us (3%)
    pallas_call x1, Pallas kernels, step(): pl.pallas_call(functools.partial(kernel, chunk, tile), name='stages', out...  236 us
    unnamed x7, local copies, waits for them, and re-layouts  7.36 us

profile of v2, /device:TPU:27, one launch (start us, length us, event | category | flops | bytes accessed | tf_op | source)
XLA Modules:
  0.0 244.0 jit_solution(6737029685981648620)
XLA Ops:
  0.6 236.0 %stages.1 = (bf16[1,512,1792]{2,1,0:T(8,128)(2,1)}, bf16[1,512,1792]{2,1,0:T(8,128)(2,1)}, bf16[1,512,1792]{2,1,0:T(8,128)(2,1)}, f32[32,2,256,1792]{3,2,1,0:T(8,128)}, bf16[16,3,512,1792]{3,2,1,0:T(8,128)(2,1)}) custom-call(bf16[16,512,512]{2,1,0:T(8,128)(2,1)} %x_ref.1, bf16[16,512,512]{2,1,0:T(8,128)(2,1)} %dy_ref.1, bf16[1,512,1792]{2,1,0:T(8,128)(2,1)} %wg_ref.1, ...), custom_call_target="tpu_custom_call" | custom-call | tf_op jit(solution)/shard_map/stages/pallas_call | solution.py:358
  236.6 0.0 copy-start.1
  236.6 4.0 %copy.8 = bf16[1,1792,512]{2,1,0:T(8,128)(2,1)} copy(bf16[1,1792,512]{1,2,0:T(8,128)(2,1)} %bitcast.1) | data formatting | bytes 3670016
  240.6 0.0 copy-done.1
  240.6 0.0 copy-start
  240.6 1.2 copy.11
  241.8 0.9 copy-done
  242.8 1.2 copy.12
Async XLA Ops:
  236.6 4.0 %copy-start.1 = (bf16[1,512,1792]{2,1,0:T(8,128)(2,1)S(1)}, bf16[1,512,1792]{2,1,0:T(8,128)(2,1)}, u32[]{:S(2)}) copy-start(bf16[1,512,1792]{2,1,0:T(8,128)(2,1)} %get-tuple-element.15) | copy-start | bytes 5505028
  240.6 2.2 copy-start
